TPU v7x, 32 devices: a whole 2x2x4 slice. The times are simulated.
32 devices in a mesh: crop: 1, dap: 32 (over z, y, x, core).
Axes of the slice: x: 2, y: 2, z: 4, core: 2. Of those that a mesh axis runs over, the one named last changes fastest.
Arguments:
- homolog_features: bfloat16 [128, 128, 256], P(('crop', 'dap')), may hold values from -6 to 6
- twofold_features: bfloat16 [128, 128, 128], P(('crop', 'dap')), may hold values from -6 to 6
- twofold_offset_map: bfloat16 [128, 8], replicated, may hold values from -0.5 to 0.5
- horizontal_attend_entry_maps: bfloat16 [256, 1024], replicated, may hold values from -2 to 2
- horizontal_attend_exit_map: bfloat16 [256, 256], replicated, may hold values from -0.375 to 0.375
- vertical_attend_entry_maps: bfloat16 [256, 1024], replicated, may hold values from -2 to 2
- vertical_attend_exit_map: bfloat16 [256, 256], replicated, may hold values from -0.375 to 0.375
- tensor_product_factors: bfloat16 [256, 64], replicated, may hold values from -0.375 to 0.375
- tensor_product_exit_map: bfloat16 [1024, 128], replicated, may hold values from -1 to 1
Outputs:
- alignment_output: bfloat16 [128, 128, 256], P('crop', 'dap')
- pair_output: bfloat16 [128, 128, 128], P(('crop', 'dap'))
All inputs are finite; a program needn't handle non-finite values.
Results may differ from a plain program's by a relative error of at most 0.0085.
Values may be sent and summed in bfloat16 or wider, within the bound.
No kernel may reach another device: no remote copies, remote signals or barrier semaphores. Data moves between devices by JAX's collectives and lax.ppermute only.
A program may use at most 64 MiB of HBM per device.

v0:
```python
import math
import jax
import jax.numpy as jnp
from jax import lax
from jax.sharding import PartitionSpec as P

EPSILON = 1e-05


def standardize_features(values):
    values = values.astype(jnp.float32)
    center = values - jnp.mean(values, axis=-1, keepdims=True)
    spread = jnp.mean(center * center, axis=-1, keepdims=True)
    return center * lax.rsqrt(spread + EPSILON)


def split_heads(packed, head_count):
    pieces = jnp.split(packed, 4, axis=-1)
    return [
        piece.reshape(piece.shape[:-1] + (head_count, piece.shape[-1] // head_count))
        for piece in pieces
    ]


def attend(queries, key_rows, value_rows, gate_rows, pair_bias):
    head_size = queries.shape[-1]
    scores = jnp.einsum(
        "bihd,bjhd->bhij", queries, key_rows, preferred_element_type=jnp.float32
    ) / math.sqrt(head_size)
    scores = scores + pair_bias
    highest = jnp.max(scores, axis=-1, keepdims=True)
    expo = jnp.exp(scores - highest)
    weights = (expo / jnp.sum(expo, axis=-1, keepdims=True)).astype(jnp.bfloat16)
    attended = jnp.einsum(
        "bhij,bjhd->bihd", weights, value_rows, preferred_element_type=jnp.float32
    )
    gated = (jax.nn.sigmoid(gate_rows.astype(jnp.float32)) * attended).astype(jnp.bfloat16)
    return gated.reshape(gated.shape[:2] + (gated.shape[2] * gated.shape[3],))


def mapped_horizontal_piece(homolog_features, horizontal_attend_entry_maps):
    horizontal_standardized = standardize_features(homolog_features).astype(jnp.bfloat16)
    return jnp.einsum(
        "src,cf->srf",
        horizontal_standardized,
        horizontal_attend_entry_maps,
        preferred_element_type=jnp.float32,
    ).astype(jnp.bfloat16)


def collect_bias(twofold_features, twofold_offset_map):
    pair_norm = standardize_features(twofold_features).astype(jnp.bfloat16)
    local_bias = jnp.einsum(
        "ijz,zh->hij", pair_norm, twofold_offset_map, preferred_element_type=jnp.float32
    ).astype(jnp.bfloat16)
    return lax.all_gather(local_bias, "dap", axis=1, tiled=True)


def column_delta(received_blocks, vertical_attend_entry_maps, vertical_attend_exit_map, head_count):
    column_alignment = received_blocks[:, 0]
    column_layer_norm = standardize_features(column_alignment).astype(jnp.bfloat16)
    col_proj = jnp.einsum(
        "skc,cf->ksf",
        column_layer_norm,
        vertical_attend_entry_maps,
        preferred_element_type=jnp.float32,
    ).astype(jnp.bfloat16)
    queries, key_rows, value_rows, gate_rows = split_heads(col_proj, head_count)
    column_gated_output = attend(queries, key_rows, value_rows, gate_rows, 0.0)
    residual_delta = jnp.einsum(
        "ksf,fc->skc",
        column_gated_output,
        vertical_attend_exit_map,
        preferred_element_type=jnp.float32,
    )
    return (column_alignment.astype(jnp.float32) + residual_delta).astype(jnp.bfloat16)


def per_device(
    homolog_features,
    twofold_features,
    twofold_offset_map,
    horizontal_attend_entry_maps,
    horizontal_attend_exit_map,
    vertical_attend_entry_maps,
    vertical_attend_exit_map,
    tensor_product_factors,
    tensor_product_exit_map,
):
    head_count = twofold_offset_map.shape[1]
    horizontal_mapped_features = mapped_horizontal_piece(
        homolog_features, horizontal_attend_entry_maps
    )
    gathered = collect_bias(twofold_features, twofold_offset_map)
    bias_wide = gathered.astype(jnp.float32)[None]
    heads_row = split_heads(horizontal_mapped_features, head_count)

    def one_sequence(items):
        return attend(items[0][None], items[1][None], items[2][None], items[3][None], bias_wide)[0]

    horizontal_sigmoid_scaled = lax.map(one_sequence, tuple(heads_row))
    homolog_line = (
        homolog_features.astype(jnp.float32)
        + jnp.einsum(
            "asd,dy->asy",
            horizontal_sigmoid_scaled,
            horizontal_attend_exit_map,
            preferred_element_type=jnp.float32,
        )
    ).astype(jnp.bfloat16)
    parallel_width = lax.axis_size("dap")
    sequence_local, residue_total, channel_count = homolog_line.shape
    alignment_blocks = homolog_line.reshape(
        sequence_local, parallel_width, residue_total // parallel_width, channel_count
    )
    alignment_output = column_delta(
        lax.all_to_all(alignment_blocks, "dap", split_axis=1, concat_axis=0, tiled=True),
        vertical_attend_entry_maps,
        vertical_attend_exit_map,
        head_count,
    )
    outer_width = tensor_product_factors.shape[1] // 2
    homolog_tally = alignment_output.shape[0]
    residue_local = alignment_output.shape[1]
    outer_layer_norm = standardize_features(alignment_output).astype(jnp.bfloat16)
    left_rows = jnp.einsum(
        "src,cf->rsf",
        outer_layer_norm,
        tensor_product_factors[:, :outer_width],
        preferred_element_type=jnp.float32,
    ).astype(jnp.bfloat16)
    right_rows = jnp.einsum(
        "src,cf->rsf",
        outer_layer_norm,
        tensor_product_factors[:, outer_width:],
        preferred_element_type=jnp.float32,
    ).astype(jnp.bfloat16)
    right_flat = right_rows.reshape(residue_local, homolog_tally * outer_width)
    segment = lax.all_gather(right_flat, "dap", axis=0, tiled=True)
    count_rows = segment.shape[0]
    right_three = segment.reshape(count_rows, homolog_tally, outer_width)
    product = (
        jnp.einsum("isc,jse->ijce", left_rows, right_three, preferred_element_type=jnp.float32)
        / homolog_tally
    )
    flat = product.astype(jnp.bfloat16).reshape(
        residue_local * count_rows, outer_width * outer_width
    )
    residual_delta = jnp.dot(flat, tensor_product_exit_map, preferred_element_type=jnp.float32)
    residual_delta = residual_delta.reshape(residue_local, count_rows, residual_delta.shape[-1])
    base_rows = twofold_features.astype(jnp.float32)
    pair_output = (base_rows + residual_delta).astype(jnp.bfloat16)
    return (alignment_output, pair_output)


def solution(mesh):
    in_specs = (
        P(("crop", "dap"), None, None),
        P(("crop", "dap"), None, None),
        P(),
        P(),
        P(),
        P(),
        P(),
        P(),
        P(),
    )
    out_specs = (P("crop", "dap", None), P(("crop", "dap"), None, None))
    return jax.shard_map(
        per_device, mesh=mesh, in_specs=in_specs, out_specs=out_specs, check_vma=False
    )
```

profile of v0, /device:TPU:0, one launch (start us, length us, event | category | flops | bytes accessed | tf_op | source)
XLA Modules:
  0.0 153.7 jit_solution(9199127318719284035)
XLA Ops:
  7.2 1.1 convert_reduce_fusion
  8.4 1.2 fusion.38
  9.6 1.4 convolution_convert_fusion.1
  12.4 0.3 fusion.32
  12.7 43.9 %all_gather.6 = bf16[8,128,128]{2,0,1:T(8,128)(2,1)S(1)} all-gather(bf16[8,4,128]{2,0,1:T(8,128)(2,1)S(1)} %fusion.32), channel_id=1, replica_groups=mesh['crop'=1,'dap'=32] {'dap'}, dimensions={1}, use_global_device_ids=true | all-gather | bytes 270336 | tf_op jit(solution)/shard_map/all_gather | solution.py:56
  56.9 3.8 %while.10 = (s32[]{:T(128)}, bf16[4,128,256]{1,2,0:T(8,128)(2,1)S(1)}, bf16[4,128,8,32]{1,3,2,0:T(8,128)(2,1)S(1)}, bf16[4,128,8,32]{1,3,2,0:T(8,128)(2,1)S(1)},...) while((s32[]{:T(128)}, ...), condition=%wide.region_7.8_spmd, body=%wide.region_4.7_spmd.sunk | while | flops 26543360 | bytes 3222617 | solution.py:101
  56.9 0.3 fusion.106
  57.2 0.4 fusion.105
  57.9 0.3 fusion.106
  58.2 0.4 fusion.105
  58.8 0.3 fusion.106
  59.1 0.4 fusion.105
  59.8 0.3 fusion.106
  60.1 0.4 fusion.105
  60.7 0.3 fusion.27
  61.2 12.3 %all_to_all.4 = bf16[4,32,4,256]{3,2,0,1:T(4,128)(2,1)S(1)} all-to-all(bf16[4,32,4,256]{3,2,0,1:T(4,128)(2,1)S(1)} %copy.80), channel_id=1, replica_groups=mesh['crop'=1,'dap'=32] {'dap'}, dimensions={1} | all-to-all | bytes 524288 | tf_op jit(solution)/shard_map/all_to_all | solution.py:117
  73.5 0.3 bitcast_reduce_fusion
  74.1 0.5 fusion.44
  75.2 0.5 fusion.22
  76.6 2.2 %fusion.81 = (f32[4,8,128]{2,1,0:T(8,128)S(1)}, f32[4,8,128,128]{2,3,1,0:T(8,128)}) fusion(bf16[4,128,8,32]{1,3,2,0:T(8,128)(2,1)S(1)} %bitcast.155, bf16[4,128,8,32]{1,3,2,0:T(8,128)(2,1)S(1)} %bitcast.156), kind=kOutput, calls=%fused_computation.102 | convolution fusion | flops 35127424 | bytes 2637824 | tf_op jit(solution)/shard_map/sub | solution.py:32
  78.9 2.0 %fusion.26 = bf16[4,128,8,32]{1,3,2,0:T(8,128)(2,1)S(1)} fusion(f32[4,128,8,32]{1,3,2,0:T(8,128)S(1)} %bitcast.152, bf16[4,128,8,32]{1,3,2,0:T(8,128)(2,1)S(1)} %bitcast.157, f32[4,8,128,128]{2,3,1,0:T(8,128)} %get-tuple-element.98, f32[4,8,128]{2,1,0:T(8,128)S(1)} %get-tuple-element.97), kind=kOutput, calls=%fused_computation.35 | convolution fusion | flops 34865152 | bytes 3162112 | tf_op jit(solution)/shard_map/bhij,bjhd->bihd/dot_general | solution.py:34
  80.9 0.4 convert_reduce_fusion.1
  81.3 0.2 fusion.40
  81.6 0.3 fusion.30
  82.0 0.8 reshape.172
  82.9 0.9 copy.99
  83.8 50.6 %all-gather.3.cloned.1.call-done = bf16[32,4,4096]{2,1,0:T(4,128)(2,1)} async-done(((bf16[1,4,4096]{2,1,0:T(4,128)(2,1)}), bf16[32,4,4096]{2,1,0:T(4,128)(2,1)}) %all-gather.3.cloned.1.call-update) | async-done | bytes 1048592 | tf_op jit(solution)/shard_map/all_gather | solution.py:139
  134.3 5.9 %reshape.165 = bf16[128,128,32]{2,1,0:T(8,128)(2,1)} reshape(bf16[32,4,4096]{2,1,0:T(4,128)(2,1)} %all-gather.3.cloned.1.call-done) | data formatting | bytes 2097152 | tf_op jit(solution)/shard_map/reshape | solution.py:141
  140.2 4.0 %copy.104 = bf16[128,128,32,1]{1,0,3,2:T(8,128)(2,1)S(1)} copy(bf16[128,128,32,1]{2,1,0,3:T(8,128)(2,1)} %bitcast.145) | data formatting | bytes 2097152 | tf_op jit(solution)/shard_map/reshape | solution.py:141
  144.2 0.7 fusion.23
  145.0 0.7 copy.97
  145.7 1.1 fusion.29
  (63 shorter events, 4.8 us)
Async XLA Ops:
  7.2 2.4 %copy-start = (bf16[256,1024]{1,0:T(8,128)(2,1)S(1)}, bf16[256,1024]{1,0:T(8,128)(2,1)}, u32[]{:S(2)}) copy-start(bf16[256,1024]{1,0:T(8,128)(2,1)} %param.14) | copy-start | bytes 1572868
  7.2 127.2 %all-gather.3.cloned.1.call-start = ((), (), s32[]{:S(2)}) async-start(), calls=%async_computation.1 | async-start | bytes 1081344 | tf_op jit(solution)/shard_map/all_gather | solution.py:139
  11.1 0.9 copy-start.2
  11.1 1.3 copy-start.8
  56.9 3.8 %copy-start.1 = (bf16[4,128,256]{2,1,0:T(8,128)(2,1)S(1)}, bf16[4,128,256]{2,1,0:T(8,128)(2,1)}, u32[]{:S(2)}) copy-start(bf16[4,128,256]{2,1,0:T(8,128)(2,1)} %param.11) | copy-start | bytes 786436
  56.9 3.8 %copy-start.5 = (bf16[256,256]{1,0:T(8,128)(2,1)S(1)}, bf16[256,256]{1,0:T(8,128)(2,1)}, u32[]{:S(2)}) copy-start(bf16[256,256]{1,0:T(8,128)(2,1)} %param.15) | copy-start | bytes 393220
  60.7 14.4 %copy-start.3 = (bf16[256,1024]{1,0:T(8,128)(2,1)S(1)}, bf16[256,1024]{1,0:T(8,128)(2,1)}, u32[]{:S(2)}) copy-start(bf16[256,1024]{1,0:T(8,128)(2,1)} %param.16) | copy-start | bytes 1572868
  78.9 2.0 %copy-start.6 = (bf16[256,256]{1,0:T(8,128)(2,1)S(1)}, bf16[256,256]{1,0:T(8,128)(2,1)}, u32[]{:S(2)}) copy-start(bf16[256,256]{1,0:T(8,128)(2,1)} %param.17) | copy-start | bytes 393220
  78.9 2.7 %copy-start.7 = (bf16[256,64]{0,1:T(8,128)(2,1)S(1)}, bf16[256,64]{0,1:T(8,128)(2,1)}, u32[]{:S(2)}) copy-start(bf16[256,64]{0,1:T(8,128)(2,1)} %param.18) | copy-start | bytes 98308
  144.2 1.4 copy-start.4
Sparse Core Ops, SparseCore 0:
  83.0 51.2 all-gather.2
where the time goes:
time: 154 us
  blocking collectives  56.2 us (36%)
  waiting for transfers between devices  50.6 us (33%)
  local copies, waits for them, and re-layouts  15.3 us (10%)
  between operations  14.4 us (9%)
  matrix products  13 us (8%)
  other arithmetic  4.06 us (3%)
    all_gather x1, waiting for transfers between devices, per_device(): segment = lax.all_gather(right_flat, 'dap', axis=0, tiled=True)  50.6 us
    all_gather x1, blocking collectives, collect_bias(): return lax.all_gather(local_bias, 'dap', axis=1, tiled=True)  43.9 us
    all_to_all x1, blocking collectives, per_device(): lax.all_to_all(alignment_blocks, 'dap', split_axis=1, concat_axis=0, tile...  12.3 us
    reshape x2, local copies, waits for them, and re-layouts, per_device(): right_three = segment.reshape(count_rows, homolog_tally, outer_width)  9.9 us
    sub x5, matrix products, attend(): expo = jnp.exp(scores - highest)  3.74 us
  transfers between devices with their start and end apart: 1, of which 1 were waited for; matrix products, arithmetic and copies ran while one was open for 1% of the time, Pallas kernels for 0%

commit v1 on v0

--- a/solution.py
+++ b/solution.py
@@ -5,6 +5,12 @@
 from jax.sharding import PartitionSpec as P
 
 EPSILON = 1e-05
+
+
+def gather_blocks(value, mesh_axis, along):
+    parts = lax.all_gather(value, mesh_axis, axis=0, tiled=False)
+    whole = jnp.concatenate(parts, axis=along)
+    return whole
 
 
 def standardize_features(values):
@@ -53,7 +59,7 @@
     local_bias = jnp.einsum(
         "ijz,zh->hij", pair_norm, twofold_offset_map, preferred_element_type=jnp.float32
     ).astype(jnp.bfloat16)
-    return lax.all_gather(local_bias, "dap", axis=1, tiled=True)
+    return gather_blocks(local_bias, "dap", 1)
 
 
 def column_delta(received_blocks, vertical_attend_entry_maps, vertical_attend_exit_map, head_count):

time: 154 us -> 154 us (level)
  no operation moved by 1% of the time
where the time goes in v1:
time: 154 us
  blocking collectives  56.2 us (36%)
  waiting for transfers between devices  50.6 us (33%)
  local copies, waits for them, and re-layouts  15.3 us (10%)
  between operations  14.4 us (9%)
  matrix products  13 us (8%)
  other arithmetic  4.06 us (3%)
    all_gather x1, waiting for transfers between devices, per_device(): segment = lax.all_gather(right_flat, 'dap', axis=0, tiled=True)  50.6 us
    all_gather x1, blocking collectives, gather_blocks(): parts = lax.all_gather(value, mesh_axis, axis=0, tiled=False)  43.9 us
    all_to_all x1, blocking collectives, per_device(): lax.all_to_all(alignment_blocks, 'dap', split_axis=1, concat_axis=0, tile...  12.3 us
    reshape x2, local copies, waits for them, and re-layouts, per_device(): right_three = segment.reshape(count_rows, homolog_tally, outer_width)  9.9 us
    sub x5, matrix products, attend(): expo = jnp.exp(scores - highest)  3.74 us
  transfers between devices with their start and end apart: 1, of which 1 were waited for; matrix products, arithmetic and copies ran while one was open for 1% of the time, Pallas kernels for 0%

profile of v1, /device:TPU:0, one launch (start us, length us, event | category | flops | bytes accessed | tf_op | source)
XLA Modules:
  0.0 153.7 jit_solution(8265886534573709663)
XLA Ops:
  7.2 1.1 convert_reduce_fusion
  8.4 1.2 fusion.38
  9.6 1.4 convolution_convert_fusion.1
  12.4 0.3 fusion.32
  12.7 43.9 %all-gather = bf16[256,4,128]{2,0,1:T(8,128)(2,1)S(1)} all-gather(bf16[8,4,128]{2,0,1:T(8,128)(2,1)S(1)} %fusion.32), channel_id=2, replica_groups=mesh['crop'=1,'dap'=32] {'dap'}, dimensions={0}, use_global_device_ids=true | all-gather | bytes 270336 | tf_op jit(solution)/shard_map/all_gather | solution.py:11
  57.0 3.8 %while.10 = (s32[]{:T(128)}, bf16[4,128,256]{1,2,0:T(8,128)(2,1)S(1)}, bf16[4,128,8,32]{1,3,2,0:T(8,128)(2,1)S(1)}, bf16[4,128,8,32]{1,3,2,0:T(8,128)(2,1)S(1)},...) while((s32[]{:T(128)}, ...), condition=%wide.region_7.8_spmd, body=%wide.region_4.7_spmd.sunk | while | flops 26543360 | bytes 3222617 | solution.py:107
  57.0 0.3 fusion.106
  57.3 0.4 fusion.105
  57.9 0.3 fusion.106
  58.2 0.4 fusion.105
  58.9 0.3 fusion.106
  59.2 0.4 fusion.105
  59.8 0.3 fusion.106
  60.1 0.4 fusion.105
  60.8 0.3 fusion.27
  61.3 12.3 %all_to_all.4 = bf16[4,32,4,256]{3,2,0,1:T(4,128)(2,1)S(1)} all-to-all(bf16[4,32,4,256]{3,2,0,1:T(4,128)(2,1)S(1)} %copy.83), channel_id=1, replica_groups=mesh['crop'=1,'dap'=32] {'dap'}, dimensions={1} | all-to-all | bytes 524288 | tf_op jit(solution)/shard_map/all_to_all | solution.py:123
  73.6 0.3 bitcast_reduce_fusion
  74.2 0.5 fusion.44
  75.2 0.5 fusion.22
  76.7 2.2 %fusion.81 = (f32[4,8,128]{2,1,0:T(8,128)S(1)}, f32[4,8,128,128]{2,3,1,0:T(8,128)}) fusion(bf16[4,128,8,32]{1,3,2,0:T(8,128)(2,1)S(1)} %bitcast.159, bf16[4,128,8,32]{1,3,2,0:T(8,128)(2,1)S(1)} %bitcast.160), kind=kOutput, calls=%fused_computation.102 | convolution fusion | flops 35127424 | bytes 2637824 | tf_op jit(solution)/shard_map/sub | solution.py:38
  79.0 2.0 %fusion.26 = bf16[4,128,8,32]{1,3,2,0:T(8,128)(2,1)S(1)} fusion(f32[4,128,8,32]{1,3,2,0:T(8,128)S(1)} %bitcast.156, bf16[4,128,8,32]{1,3,2,0:T(8,128)(2,1)S(1)} %bitcast.161, f32[4,8,128,128]{2,3,1,0:T(8,128)} %get-tuple-element.98, f32[4,8,128]{2,1,0:T(8,128)S(1)} %get-tuple-element.97), kind=kOutput, calls=%fused_computation.35 | convolution fusion | flops 34865152 | bytes 3162112 | tf_op jit(solution)/shard_map/bhij,bjhd->bihd/dot_general | solution.py:40
  81.0 0.4 convert_reduce_fusion.1
  81.4 0.2 fusion.40
  81.6 0.3 fusion.30
  82.1 0.8 reshape.188
  82.9 0.9 copy.102
  83.8 50.6 %all-gather.4.cloned.1.call-done = bf16[32,4,4096]{2,1,0:T(4,128)(2,1)} async-done(((bf16[1,4,4096]{2,1,0:T(4,128)(2,1)}), bf16[32,4,4096]{2,1,0:T(4,128)(2,1)}) %all-gather.4.cloned.1.call-update) | async-done | bytes 1048592 | tf_op jit(solution)/shard_map/all_gather | solution.py:145
  134.4 5.9 %reshape.179 = bf16[128,128,32]{2,1,0:T(8,128)(2,1)} reshape(bf16[32,4,4096]{2,1,0:T(4,128)(2,1)} %all-gather.4.cloned.1.call-done) | data formatting | bytes 2097152 | tf_op jit(solution)/shard_map/reshape | solution.py:147
  140.3 4.0 %copy.107 = bf16[128,128,32,1]{1,0,3,2:T(8,128)(2,1)S(1)} copy(bf16[128,128,32,1]{2,1,0,3:T(8,128)(2,1)} %bitcast.148) | data formatting | bytes 2097152 | tf_op jit(solution)/shard_map/reshape | solution.py:147
  144.3 0.7 fusion.23
  145.0 0.7 copy.100
  145.7 1.1 fusion.29
  (64 shorter events, 4.8 us)
Async XLA Ops:
  7.2 2.4 %copy-start = (bf16[256,1024]{1,0:T(8,128)(2,1)S(1)}, bf16[256,1024]{1,0:T(8,128)(2,1)}, u32[]{:S(2)}) copy-start(bf16[256,1024]{1,0:T(8,128)(2,1)} %param.14) | copy-start | bytes 1572868
  7.2 127.2 %all-gather.4.cloned.1.call-start = ((), (), s32[]{:S(2)}) async-start(), calls=%async_computation.1 | async-start | bytes 1081344 | tf_op jit(solution)/shard_map/all_gather | solution.py:145
  11.1 0.9 copy-start.2
  11.1 1.3 copy-start.8
  57.0 3.8 %copy-start.1 = (bf16[4,128,256]{2,1,0:T(8,128)(2,1)S(1)}, bf16[4,128,256]{2,1,0:T(8,128)(2,1)}, u32[]{:S(2)}) copy-start(bf16[4,128,256]{2,1,0:T(8,128)(2,1)} %param.11) | copy-start | bytes 786436
  57.0 3.8 %copy-start.5 = (bf16[256,256]{1,0:T(8,128)(2,1)S(1)}, bf16[256,256]{1,0:T(8,128)(2,1)}, u32[]{:S(2)}) copy-start(bf16[256,256]{1,0:T(8,128)(2,1)} %param.15) | copy-start | bytes 393220
  60.8 14.4 %copy-start.3 = (bf16[256,1024]{1,0:T(8,128)(2,1)S(1)}, bf16[256,1024]{1,0:T(8,128)(2,1)}, u32[]{:S(2)}) copy-start(bf16[256,1024]{1,0:T(8,128)(2,1)} %param.16) | copy-start | bytes 1572868
  78.9 2.0 %copy-start.6 = (bf16[256,256]{1,0:T(8,128)(2,1)S(1)}, bf16[256,256]{1,0:T(8,128)(2,1)}, u32[]{:S(2)}) copy-start(bf16[256,256]{1,0:T(8,128)(2,1)} %param.17) | copy-start | bytes 393220
  79.0 2.7 %copy-start.7 = (bf16[256,64]{0,1:T(8,128)(2,1)S(1)}, bf16[256,64]{0,1:T(8,128)(2,1)}, u32[]{:S(2)}) copy-start(bf16[256,64]{0,1:T(8,128)(2,1)} %param.18) | copy-start | bytes 98308
  144.3 1.4 copy-start.4
Sparse Core Ops, SparseCore 0:
  83.1 51.2 all-gather.3
